TPU v7x, 32 devices: a whole 2x2x4 slice. The times are simulated.
32 devices in a mesh: curve: 16 (over z, y, core), tm: 2 (over x).
Axes of the slice: x: 2, y: 2, z: 4, core: 2. Of those that a mesh axis runs over, the one named last changes fastest.
Arguments:
- samples: float32 [4096, 65536], P('curve', 'tm'), may hold values from -30 to 30
- smoothing: float32 [4096], P('curve'), may hold values from 0.5 to 20
- test_matrix: float32 [4096, 64], P('tm'), may hold values from -0.75 to 0.75
- sketch_prev: float32 [4096, 64], P('tm', 'curve'), may hold values from -1.2 to 1.2
Outputs:
- coefficients: float32 [4096, 4096], P('curve', 'tm')
- scores: float32 [4096, 64], P('curve')
- sketch: float32 [4096, 64], P('tm', 'curve')
All inputs are finite; a program needn't handle non-finite values.
Results may differ from a plain program's by a relative error of at most 0.0002.
Values sent between devices are 32-bit elements; how exact they have to be, the bound alone decides.
No kernel may reach another device: no remote copies, remote signals or barrier semaphores. Data moves between devices by JAX's collectives and lax.ppermute only.
A program may use at most 192 MiB of HBM per device.

v0:
```python
import jax
import jax.numpy as jnp
from jax import lax
from jax.sharding import PartitionSpec as P

SPB = 16
ITERS = 4
damping = 0.45


def passed_along(block, axis, distance):
    devices = range(lax.axis_size(axis))
    route = [(i - distance, i) for i in devices if i - distance in devices]
    return lax.ppermute(block, axis, route)


def padded_2(block, sides, width):
    for axis, dim in sides:
        count = lax.axis_size(axis)
        forward = [(i, i + 1) for i in range(count - 1)]
        backward = [(target, source) for source, target in forward]
        low = lax.ppermute(
            lax.slice_in_dim(block, block.shape[dim] - width, None, axis=dim), axis, forward
        )
        high = lax.ppermute(lax.slice_in_dim(block, 0, width, axis=dim), axis, backward)
        block = jnp.concatenate([low, block, high], axis=dim)
    return block


def weight_table():
    frac = (jnp.arange(SPB, dtype=jnp.float32) + 0.5) / SPB
    pieces = [
        frac**3 / 6.0,
        (-3.0 * frac**3 + 3.0 * frac**2 + 3.0 * frac + 1.0) / 6.0,
        (3.0 * frac**3 - 6.0 * frac**2 + 4.0) / 6.0,
        (1.0 - frac) ** 3 / 6.0,
    ]
    return jnp.stack(pieces) / SPB


def relax_sweep(widened, target, smooth_col, index_wide, total_basis):
    second = widened[:, 2:] - 2.0 * widened[:, 1:-1] + widened[:, :-2]
    in_range = (index_wide[:-2] >= 0) & (index_wide[:-2] <= total_basis - 3)
    second = jnp.where(in_range[None, :], second, 0.0)
    bending = second[:, 2:] - 2.0 * second[:, 1:-1] + second[:, :-2]
    interior = widened[:, 2:-2]
    column_index = index_wide[2:-2]
    penalty_diag = (
        (column_index <= total_basis - 3).astype(jnp.float32)
        + 4.0 * ((column_index >= 1) & (column_index <= total_basis - 2)).astype(jnp.float32)
        + (column_index >= 2).astype(jnp.float32)
    )
    return interior + damping * (target - interior - smooth_col * bending) / (
        1.0 + smooth_col * penalty_diag
    )


def body(samples, smoothing, test_matrix, sketch_prev):
    row_count = samples.shape[0]
    basis_width = samples.shape[1] // SPB
    blocks = samples.reshape(row_count, basis_width, SPB)
    segment_sums = jnp.einsum(
        "cgq,mq->mcg", blocks, weight_table(), precision=lax.Precision.HIGHEST
    )
    padded = jnp.pad(segment_sums, ((0, 0), (0, 0), (3, 3)))
    extended = (
        padded[0, :, 0 : basis_width + 3]
        + padded[1, :, 1 : basis_width + 4]
        + padded[2, :, 2 : basis_width + 5]
        + padded[3, :, 3 : basis_width + 6]
    )
    spilled = extended[:, basis_width:]
    arrived = passed_along(spilled, "tm", 1)
    proj = jnp.concatenate([extended[:, :3] + arrived, extended[:, 3:basis_width]], axis=1)
    total_basis = basis_width * lax.axis_size("tm")
    first_column = lax.axis_index("tm") * basis_width
    smooth_col = smoothing[:, None]
    margin = 2 * ITERS
    proj_wide = padded_2(proj, (("tm", 1),), margin)
    coefficients = proj_wide
    for sweep_number in range(ITERS):
        margin_now = margin - 2 * sweep_number
        index_wide = (
            first_column - margin_now + jnp.arange(basis_width + 2 * margin_now, dtype=jnp.int32)
        )
        offset = 2 * sweep_number + 2
        target = proj_wide[:, offset : offset + basis_width + 2 * margin_now - 4]
        coefficients = relax_sweep(coefficients, target, smooth_col, index_wide, total_basis)
    curve_total = row_count * lax.axis_size("curve")
    totals = lax.psum(jnp.sum(coefficients, axis=0), "curve")
    column_mean = totals / curve_total
    centered = coefficients - column_mean[None, :]
    partial_value = jnp.dot(
        centered, test_matrix, precision=lax.Precision.HIGHEST, preferred_element_type=jnp.float32
    )
    scores = lax.psum(partial_value, "tm")
    sketch_part = (
        jnp.einsum("ck,cr->kr", centered, scores, precision=lax.Precision.HIGHEST) / curve_total
    )
    owned_part = lax.psum_scatter(sketch_part, "curve", scatter_dimension=1, tiled=True)
    return (coefficients, scores, sketch_prev + owned_part)


def solution(mesh):
    placed = (P("curve", "tm"), P("curve"), P("tm", None), P("tm", "curve"))
    return jax.shard_map(
        body,
        mesh=mesh,
        in_specs=placed,
        out_specs=(P("curve", "tm"), P("curve", None), P("tm", "curve")),
        check_vma=False,
    )
```

profile of v0, /device:TPU:0, one launch (start us, length us, event | category | flops | bytes accessed | tf_op | source)
XLA Modules:
  0.0 307.5 jit_solution(17813712295289506983)
XLA Ops:
  7.2 0.0 copy-start
  7.2 0.0 all-reduce.5.cloned.1.call-start
  7.3 33.5 %copy.12 = f32[256,32768]{0,1:T(8,128)} copy(f32[256,32768]{1,0:T(8,128)} %param.4) | data formatting | bytes 67108864 | tf_op args[0]
  40.7 35.7 %copy.13 = f32[256,2048,16]{1,2,0:T(8,128)} copy(f32[256,2048,16]{0,2,1:T(8,128)} %bitcast.9) | data formatting | bytes 67108864 | tf_op jit(solution)/shard_map/reshape | solution.py:61
  76.4 21.7 %fusion.43 = f32[4,256,2048]{2,0,1:T(4,128)S(1)} fusion(f32[256,2048,16]{1,2,0:T(8,128)} %copy.13, f32[1,16]{1,0:T(1,128)S(1)} %get-tuple-element.11, f32[1,16]{1,0:T(1,128)S(1)} %get-tuple-element.12, f32[1,16]{1,0:T(1,128)S(1)} %get-tuple-element.13, f32[1,16]{1,0:T(1,128)S(1)} %get-tuple-element.14), kind=kOutput, calls=%fused_computation.85 | convolution fusion | flops 402653440 | bytes 41943296 | tf_op jit(solution)/shard_map/cgq,mq->mcg/dot_general | solution.py:62
  98.1 16.1 %fusion.2 = f32[1,256,2051]{2,0,1:T(1,128)S(1)} fusion(f32[4,256,2048]{2,0,1:T(4,128)S(1)} %fusion.43), kind=kLoop, calls=%fused_computation.9 | loop fusion | flops 1575168 | bytes 10488832 | tf_op jit(solution)/shard_map/add | solution.py:67
  114.3 4.1 %copy.14 = f32[1,256,2051]{1,2,0:T(8,128)} copy(f32[1,256,2051]{2,0,1:T(1,128)S(1)} %fusion.2) | data formatting | bytes 4200448 | tf_op jit(solution)/shard_map/add | solution.py:67
  118.4 0.7 slice.196
  119.1 4.9 %collective-permute-start.1 = (f32[256,3]{0,1:T(4,128)S(1)}, f32[256,3]{0,1:T(4,128)S(1)}, u32[]{:S(2)}, u32[]{:S(2)}) collective-permute-start(f32[256,3]{0,1:T(4,128)S(1)} %slice.196), channel_id=1, source_target_pairs={{0,1},{2,3},{4,5},{6,7},{8,9},{10,11},{12,13},{14,15},{16,17},{18,... | collective-permute-start | bytes 9224 | tf_op jit(solution)/shard_map/ppermute | solution.py:14
  124.0 0.7 slice.194
  124.7 1.3 collective-permute-start
  126.0 0.1 convert_add_fusion.2
  126.1 0.1 convert_add_fusion.1
  126.2 0.1 convert_add_fusion
  126.3 0.1 convert_add_fusion.3
  126.3 1.7 slice.197
  128.1 0.0 copy-start.1
  128.1 0.0 collective-permute-done.1
  128.1 0.7 slice_add_fusion.8
  128.9 1.5 collective-permute-start.2
  130.3 0.0 collective-permute-done
  130.4 0.0 copy-done.1
  130.4 4.0 %collective-permute-done.2 = f32[256,8]{0,1:T(8,128)S(1)} collective-permute-done((f32[256,8]{0,1:T(8,128)S(1)}, f32[256,8]{0,1:T(8,128)S(1)}, u32[]{:S(2)}, u32[]{:S(2)}) %collective-permute-start.2) | collective-permute-done | bytes 8224 | tf_op jit(solution)/shard_map/ppermute | solution.py:25
  134.4 5.3 %concatenate.8 = f32[256,2064]{0,1:T(8,128)S(1)} concatenate(f32[256,8]{0,1:T(8,128)S(1)} %collective-permute-done, f32[256,3]{0,1:T(4,128)S(1)} %slice_add_fusion.8, f32[256,2045]{0,1:T(8,128)} %copy-done.1, f32[256,8]{0,1:T(8,128)S(1)} %collective-permute-done.2), dimensions={1} | concatenate | bytes 4227072 | tf_op jit(solution)/shard_map/concatenate | solution.py:26
  139.7 0.0 copy-start.5
  139.7 1.2 fusion.11
  140.9 0.0 copy-done.5
  140.9 1.7 fusion.9
  142.6 1.2 fusion.3
  143.8 1.8 fusion.27
  145.6 1.2 fusion.21
  146.8 1.8 fusion.19
  148.6 0.0 copy-start.2
  148.6 1.2 fusion.13
  149.8 0.4 copy-done.2
  150.2 1.8 fusion.56
  152.1 32.6 %psum.14 = f32[2048]{0:T(1024)S(1)} all-reduce(f32[2048]{0:T(1024)S(1)} %get-tuple-element.9), channel_id=1, replica_groups=mesh['curve'=16,'tm'=2] {'curve'}, use_global_device_ids=true, to_apply=%region_1.2 | all-reduce | flops 2048 | bytes 16384 | tf_op jit(solution)/shard_map/psum | solution.py:90
  184.6 0.0 copy-done
  184.6 2.1 fusion.37
  186.8 0.0 copy-start.6
  186.8 0.0 all-reduce.5.cloned.1.call-update
  186.8 0.0 all-reduce.7.cloned.1.call-start
  186.8 16.9 %all-reduce.5.cloned.1.call-done = f32[256,64]{0,1:T(8,128)} async-done(((f32[256,64]{0,1:T(8,128)}), f32[256,64]{0,1:T(8,128)}) %all-reduce.5.cloned.1.call-update) | async-done | bytes 65552 | tf_op jit(solution)/shard_map/psum | solution.py:96
  203.8 3.9 %convolution_multiply_fusion = f32[2048,64]{0,1:T(8,128)} fusion(f32[256,64]{0,1:T(8,128)} %all-reduce.5.cloned.1.call-done, f32[256,2048]{0,1:T(8,128)S(1)} %get-tuple-element.10, f32[2048]{0:T(1024)S(1)} %broadcast_multiply_fusion), kind=kOutput, calls=%fused_computation.6 | convolution fusion | flops 403308544 | bytes 2695168 | tf_op jit(solution)/shard_map/ck,cr->kr/dot_general | solution.py:98
  207.7 0.0 all-reduce.7.cloned.1.call-update
  207.7 0.0 copy-start.4
  207.7 0.0 copy-done.6
  207.7 0.6 dynamic-slice
  209.0 0.0 copy-start.3
  209.0 1.8 copy.15
  210.8 87.7 %all-reduce.7.cloned.1.call-done = f32[2048,64]{0,1:T(8,128)} async-done(((f32[2048,64]{0,1:T(8,128)}), f32[2048,64]{0,1:T(8,128)}) %all-reduce.7.cloned.1.call-update) | async-done | bytes 524304
  298.5 0.0 copy-done.4
  298.5 1.5 dynamic-slice_add_fusion
  300.0 0.0 copy-done.3
  300.0 0.6 copy.18
  (12 shorter events, 0.1 us)
Async XLA Ops:
  7.2 177.5 %copy-start = (f32[2048,64]{0,1:T(8,128)S(1)}, f32[2048,64]{0,1:T(8,128)}, u32[]{:S(2)}) copy-start(f32[2048,64]{0,1:T(8,128)} %param.6) | copy-start | bytes 1572868
  7.2 196.6 %all-reduce.5.cloned.1.call-start = ((), (), s32[]{:S(2)}) async-start(), calls=%async_computation | async-start | bytes 131072 | tf_op jit(solution)/shard_map/psum | solution.py:96
  119.1 9.0 %collective-permute-start.1 = (f32[256,3]{0,1:T(4,128)S(1)}, f32[256,3]{0,1:T(4,128)S(1)}, u32[]{:S(2)}, u32[]{:S(2)}) collective-permute-start(f32[256,3]{0,1:T(4,128)S(1)} %slice.196), channel_id=1, source_target_pairs={{0,1},{2,3},{4,5},{6,7},{8,9},{10,11},{12,13},{14,15},{16,17},{18,... | collective-permute-start | bytes 9224 | tf_op jit(solution)/shard_map/ppermute | solution.py:14
  124.7 5.7 %collective-permute-start = (f32[256,8]{0,1:T(8,128)S(1)}, f32[256,8]{0,1:T(8,128)S(1)}, u32[]{:S(2)}, u32[]{:S(2)}) collective-permute-start(f32[256,8]{0,1:T(8,128)S(1)} %slice.194), channel_id=1, source_target_pairs={{0,1},{2,3},{4,5},{6,7},{8,9},{10,11},{12,13},{14,15},{16,17},{18,... | collective-permute-start | bytes 24584 | tf_op jit(solution)/shard_map/ppermute | solution.py:22
  128.1 2.3 copy-start.1
  128.9 5.5 %collective-permute-start.2 = (f32[256,8]{0,1:T(8,128)S(1)}, f32[256,8]{0,1:T(8,128)S(1)}, u32[]{:S(2)}, u32[]{:S(2)}) collective-permute-start(f32[256,8]{0,1:T(8,128)S(1)} %fusion.41), channel_id=1, source_target_pairs={{1,0},{3,2},{5,4},{7,6},{9,8},{11,10},{13,12},{15,14},{17,16},{19,... | collective-permute-start | bytes 24584 | tf_op jit(solution)/shard_map/ppermute | solution.py:25
  139.7 1.2 copy-start.5
  148.6 1.6 copy-start.2
  186.8 21.0 %copy-start.6 = (u32[32]{0:T(128)S(1)}, u32[32]{0:T(128)}, u32[]{:S(2)}) copy-start(u32[32]{0:T(128)} %constant.48) | copy-start | bytes 388
  186.8 111.7 %all-reduce.7.cloned.1.call-start = ((), (), s32[]{:S(2)}) async-start(), calls=%async_computation.1 | async-start | bytes 1048576
  207.7 90.8 %copy-start.4 = (f32[2048,4]{0,1:T(4,128)S(1)}, f32[2048,4]{0,1:T(4,128)}, u32[]{:S(2)}) copy-start(f32[2048,4]{0,1:T(4,128)} %param.7) | copy-start | bytes 98308
  209.0 91.0 %copy-start.3 = (f32[256,64]{0,1:T(8,128)S(1)}, f32[256,64]{0,1:T(8,128)}, u32[]{:S(2)}) copy-start(f32[256,64]{0,1:T(8,128)} %all-reduce.5.cloned.1.call-done) | copy-start | bytes 196612
Sparse Core Ops, SparseCore 0:
  186.9 16.7 all-reduce.4
  207.8 90.6 all-reduce.6
where the time goes:
time: 309 us; the launch traced here: 307 us
  waiting for transfers between devices  109 us (35%)
  local copies, waits for them, and re-layouts  85.2 us (28%)
  blocking collectives  32.6 us (11%)
  other arithmetic  30.6 us (10%)
  matrix products  27.7 us (9%)
  between operations  15 us (5%)
  starting transfers between devices  7.68 us (2%)
    unnamed x3, waiting for transfers between devices  87.8 us
    unnamed x18, local copies, waits for them, and re-layouts  36.9 us
    reshape x1, local copies, waits for them, and re-layouts, body(): blocks = samples.reshape(row_count, basis_width, SPB)  35.7 us
    psum x1, blocking collectives, body(): totals = lax.psum(jnp.sum(coefficients, axis=0), 'curve')  32.6 us
    dot_general x1, matrix products, body(): jnp.einsum('cgq,mq->mcg', blocks, weight_table(), precision=lax.Precision...  21.7 us
    psum x1, waiting for transfers between devices, body(): scores = lax.psum(partial_value, 'tm')  16.9 us
    add x1, other arithmetic, body(): padded[0, :, 0:basis_width + 3] + padded[1, :, 1:basis_width + 4]  16.1 us
  transfers between devices with their start and end apart: 5, of which 3 were waited for; matrix products, arithmetic and copies ran while one was open for 2% of the time, Pallas kernels for 0%

commit v1 on v0

--- a/solution.py
+++ b/solution.py
@@ -87,7 +87,9 @@
         target = proj_wide[:, offset : offset + basis_width + 2 * margin_now - 4]
         coefficients = relax_sweep(coefficients, target, smooth_col, index_wide, total_basis)
     curve_total = row_count * lax.axis_size("curve")
-    totals = lax.psum(jnp.sum(coefficients, axis=0), "curve")
+    own = jnp.sum(coefficients, axis=0)
+    parts = lax.all_gather(own, "curve", axis=0, tiled=False)
+    totals = parts.sum(axis=0)
     column_mean = totals / curve_total
     centered = coefficients - column_mean[None, :]
     partial_value = jnp.dot(

time: 309 us -> 299 us (0.968)
  blocking collectives: 32.6 us -> 22 us
    psum x1 -> x0, blocking collectives: 32.6 us -> none  [body(): totals = lax.psum(jnp.sum(coefficients, axis=0), 'curve')]
    all_gather x0 -> x1, blocking collectives: none -> 22 us  [body(): parts = lax.all_gather(own, 'curve', axis=0, tiled=False)]
where the time goes in v1:
time: 299 us; the launch traced here: 297 us
  waiting for transfers between devices  109 us (36%)
  local copies, waits for them, and re-layouts  85.2 us (28%)
  other arithmetic  30.7 us (10%)
  matrix products  27.7 us (9%)
  blocking collectives  22 us (7%)
  between operations  15 us (5%)
  starting transfers between devices  7.68 us (3%)
    unnamed x3, waiting for transfers between devices  87.8 us
    unnamed x18, local copies, waits for them, and re-layouts  36.9 us
    reshape x1, local copies, waits for them, and re-layouts, body(): blocks = samples.reshape(row_count, basis_width, SPB)  35.7 us
    all_gather x1, blocking collectives, body(): parts = lax.all_gather(own, 'curve', axis=0, tiled=False)  22 us
    dot_general x1, matrix products, body(): jnp.einsum('cgq,mq->mcg', blocks, weight_table(), precision=lax.Precision...  21.7 us
    psum x1, waiting for transfers between devices, body(): scores = lax.psum(partial_value, 'tm')  17.2 us
    add x1, other arithmetic, body(): padded[0, :, 0:basis_width + 3] + padded[1, :, 1:basis_width + 4]  16.1 us
  transfers between devices with their start and end apart: 5, of which 3 were waited for; matrix products, arithmetic and copies ran while one was open for 2% of the time, Pallas kernels for 0%

profile of v1, /device:TPU:0, one launch (start us, length us, event | category | flops | bytes accessed | tf_op | source)
XLA Modules:
  0.0 297.2 jit_solution(15883552816267919948)
XLA Ops:
  7.2 0.0 copy-start
  7.2 0.0 all-reduce.5.cloned.1.call-start
  7.3 33.5 %copy.16 = f32[256,32768]{0,1:T(8,128)} copy(f32[256,32768]{1,0:T(8,128)} %param.4) | data formatting | bytes 67108864 | tf_op args[0]
  40.7 35.7 %copy.17 = f32[256,2048,16]{1,2,0:T(8,128)} copy(f32[256,2048,16]{0,2,1:T(8,128)} %bitcast.9) | data formatting | bytes 67108864 | tf_op jit(solution)/shard_map/reshape | solution.py:61
  76.4 21.7 %fusion.43 = f32[4,256,2048]{2,0,1:T(4,128)S(1)} fusion(f32[256,2048,16]{1,2,0:T(8,128)} %copy.17, f32[1,16]{1,0:T(1,128)S(1)} %get-tuple-element.14, f32[1,16]{1,0:T(1,128)S(1)} %get-tuple-element.15, f32[1,16]{1,0:T(1,128)S(1)} %get-tuple-element.16, f32[1,16]{1,0:T(1,128)S(1)} %get-tuple-element.17), kind=kOutput, calls=%fused_computation.85 | convolution fusion | flops 402653440 | bytes 41943296 | tf_op jit(solution)/shard_map/cgq,mq->mcg/dot_general | solution.py:62
  98.1 16.1 %fusion.2 = f32[1,256,2051]{2,0,1:T(1,128)S(1)} fusion(f32[4,256,2048]{2,0,1:T(4,128)S(1)} %fusion.43), kind=kLoop, calls=%fused_computation.9 | loop fusion | flops 1575168 | bytes 10488832 | tf_op jit(solution)/shard_map/add | solution.py:67
  114.3 4.1 %copy.18 = f32[1,256,2051]{1,2,0:T(8,128)} copy(f32[1,256,2051]{2,0,1:T(1,128)S(1)} %fusion.2) | data formatting | bytes 4200448 | tf_op jit(solution)/shard_map/add | solution.py:67
  118.4 0.7 slice.196
  119.1 4.9 %collective-permute-start.1 = (f32[256,3]{0,1:T(4,128)S(1)}, f32[256,3]{0,1:T(4,128)S(1)}, u32[]{:S(2)}, u32[]{:S(2)}) collective-permute-start(f32[256,3]{0,1:T(4,128)S(1)} %slice.196), channel_id=1, source_target_pairs={{0,1},{2,3},{4,5},{6,7},{8,9},{10,11},{12,13},{14,15},{16,17},{18,... | collective-permute-start | bytes 9224 | tf_op jit(solution)/shard_map/ppermute | solution.py:14
  124.0 0.7 slice.194
  124.7 1.3 collective-permute-start
  126.0 0.1 convert_add_fusion.2
  126.1 0.1 convert_add_fusion.1
  126.2 0.1 convert_add_fusion
  126.3 0.1 convert_add_fusion.3
  126.3 1.7 slice.197
  128.1 0.0 copy-start.1
  128.1 0.0 collective-permute-done.1
  128.1 0.7 slice_add_fusion.8
  128.9 1.5 collective-permute-start.2
  130.3 0.0 collective-permute-done
  130.4 0.0 copy-done.1
  130.4 4.0 %collective-permute-done.2 = f32[256,8]{0,1:T(8,128)S(1)} collective-permute-done((f32[256,8]{0,1:T(8,128)S(1)}, f32[256,8]{0,1:T(8,128)S(1)}, u32[]{:S(2)}, u32[]{:S(2)}) %collective-permute-start.2) | collective-permute-done | bytes 8224 | tf_op jit(solution)/shard_map/ppermute | solution.py:25
  134.4 5.3 %concatenate.8 = f32[256,2064]{0,1:T(8,128)S(1)} concatenate(f32[256,8]{0,1:T(8,128)S(1)} %collective-permute-done, f32[256,3]{0,1:T(4,128)S(1)} %slice_add_fusion.8, f32[256,2045]{0,1:T(8,128)} %copy-done.1, f32[256,8]{0,1:T(8,128)S(1)} %collective-permute-done.2), dimensions={1} | concatenate | bytes 4227072 | tf_op jit(solution)/shard_map/concatenate | solution.py:26
  139.7 0.0 copy-start.5
  139.7 1.2 fusion.11
  140.9 0.0 copy-done.5
  140.9 1.7 fusion.9
  142.6 1.2 fusion.3
  143.8 1.8 fusion.27
  145.6 1.2 fusion.21
  146.8 1.8 fusion.19
  148.6 0.0 copy-start.2
  148.6 1.2 fusion.13
  149.8 0.4 copy-done.2
  150.2 1.8 fusion.56
  152.1 22.0 %all-gather = f32[32768]{0:T(1024)S(1)} all-gather(f32[2048]{0:T(1024)S(1)} %get-tuple-element.12), channel_id=2, replica_groups=mesh['curve'=16,'tm'=2] {'curve'}, dimensions={0}, use_global_device_ids=true | all-gather | bytes 139264 | tf_op jit(solution)/shard_map/all_gather | solution.py:91
  174.1 0.0 copy-done
  174.1 2.1 fusion.37
  176.3 0.0 copy-start.6
  176.3 0.0 all-reduce.5.cloned.1.call-update
  176.3 0.0 all-reduce.7.cloned.1.call-start
  176.3 17.2 %all-reduce.5.cloned.1.call-done = f32[256,64]{0,1:T(8,128)} async-done(((f32[256,64]{0,1:T(8,128)}), f32[256,64]{0,1:T(8,128)}) %all-reduce.5.cloned.1.call-update) | async-done | bytes 65552 | tf_op jit(solution)/shard_map/psum | solution.py:98
  193.5 3.9 %convolution_multiply_fusion = f32[2048,64]{0,1:T(8,128)} fusion(f32[256,64]{0,1:T(8,128)} %all-reduce.5.cloned.1.call-done, f32[256,2048]{0,1:T(8,128)S(1)} %get-tuple-element.13, f32[2048]{0:T(1024)S(1)} %broadcast_multiply_fusion), kind=kOutput, calls=%fused_computation.6 | convolution fusion | flops 403308544 | bytes 2695168 | tf_op jit(solution)/shard_map/ck,cr->kr/dot_general | solution.py:100
  197.4 0.0 all-reduce.7.cloned.1.call-update
  197.5 0.0 copy-start.4
  197.5 0.0 copy-done.6
  197.5 0.6 dynamic-slice
  198.7 0.0 copy-start.3
  198.7 1.8 copy.19
  200.5 87.7 %all-reduce.7.cloned.1.call-done = f32[2048,64]{0,1:T(8,128)} async-done(((f32[2048,64]{0,1:T(8,128)}), f32[2048,64]{0,1:T(8,128)}) %all-reduce.7.cloned.1.call-update) | async-done | bytes 524304
  288.3 0.0 copy-done.4
  288.3 1.5 dynamic-slice_add_fusion
  289.7 0.0 copy-done.3
  289.7 0.6 copy.22
  (14 shorter events, 0.1 us)
Async XLA Ops:
  7.2 167.0 %copy-start = (f32[2048,64]{0,1:T(8,128)S(1)}, f32[2048,64]{0,1:T(8,128)}, u32[]{:S(2)}) copy-start(f32[2048,64]{0,1:T(8,128)} %param.6) | copy-start | bytes 1572868
  7.2 186.3 %all-reduce.5.cloned.1.call-start = ((), (), s32[]{:S(2)}) async-start(), calls=%async_computation | async-start | bytes 131072 | tf_op jit(solution)/shard_map/psum | solution.py:98
  119.1 9.0 %collective-permute-start.1 = (f32[256,3]{0,1:T(4,128)S(1)}, f32[256,3]{0,1:T(4,128)S(1)}, u32[]{:S(2)}, u32[]{:S(2)}) collective-permute-start(f32[256,3]{0,1:T(4,128)S(1)} %slice.196), channel_id=1, source_target_pairs={{0,1},{2,3},{4,5},{6,7},{8,9},{10,11},{12,13},{14,15},{16,17},{18,... | collective-permute-start | bytes 9224 | tf_op jit(solution)/shard_map/ppermute | solution.py:14
  124.7 5.7 %collective-permute-start = (f32[256,8]{0,1:T(8,128)S(1)}, f32[256,8]{0,1:T(8,128)S(1)}, u32[]{:S(2)}, u32[]{:S(2)}) collective-permute-start(f32[256,8]{0,1:T(8,128)S(1)} %slice.194), channel_id=1, source_target_pairs={{0,1},{2,3},{4,5},{6,7},{8,9},{10,11},{12,13},{14,15},{16,17},{18,... | collective-permute-start | bytes 24584 | tf_op jit(solution)/shard_map/ppermute | solution.py:22
  128.1 2.3 copy-start.1
  128.9 5.5 %collective-permute-start.2 = (f32[256,8]{0,1:T(8,128)S(1)}, f32[256,8]{0,1:T(8,128)S(1)}, u32[]{:S(2)}, u32[]{:S(2)}) collective-permute-start(f32[256,8]{0,1:T(8,128)S(1)} %fusion.41), channel_id=1, source_target_pairs={{1,0},{3,2},{5,4},{7,6},{9,8},{11,10},{13,12},{15,14},{17,16},{19,... | collective-permute-start | bytes 24584 | tf_op jit(solution)/shard_map/ppermute | solution.py:25
  139.7 1.2 copy-start.5
  148.6 1.6 copy-start.2
  176.3 21.2 %copy-start.6 = (u32[32]{0:T(128)S(1)}, u32[32]{0:T(128)}, u32[]{:S(2)}) copy-start(u32[32]{0:T(128)} %constant.48) | copy-start | bytes 388
  176.3 112.0 %all-reduce.7.cloned.1.call-start = ((), (), s32[]{:S(2)}) async-start(), calls=%async_computation.1 | async-start | bytes 1048576
  197.5 90.8 %copy-start.4 = (f32[2048,4]{0,1:T(4,128)S(1)}, f32[2048,4]{0,1:T(4,128)}, u32[]{:S(2)}) copy-start(f32[2048,4]{0,1:T(4,128)} %param.7) | copy-start | bytes 98308
  198.7 91.0 %copy-start.3 = (f32[256,64]{0,1:T(8,128)S(1)}, f32[256,64]{0,1:T(8,128)}, u32[]{:S(2)}) copy-start(f32[256,64]{0,1:T(8,128)} %all-reduce.5.cloned.1.call-done) | copy-start | bytes 196612
Sparse Core Ops, SparseCore 0:
  176.4 17.0 all-reduce.4
  197.6 90.6 all-reduce.6
